TPU v7x, 32 devices: a whole 2x2x4 slice. The times are simulated.
32 devices in a mesh: row: 4 (over y, x), col: 8 (over z, core).
Axes of the slice: x: 2, y: 2, z: 4, core: 2. Of those that a mesh axis runs over, the one named last changes fastest.
Arguments:
- start_vector: bfloat16 [4, 2048, 2048], P(None, 'row', 'col'), may hold values from -150 to 150
- left_env: bfloat16 [5, 2048, 2048], P(None, 'row', 'col'), may hold values from -5 to 6
- right_env: bfloat16 [5, 2048, 2048], P(None, 'col', 'row'), may hold values from -5 to 6
- left_tensor: float32 [5, 5, 2, 2], replicated, may hold values from -1.5 to 2.5
- right_tensor: float32 [5, 5, 2, 2], replicated, may hold values from -1.5 to 2.5
Outputs:
- next_vector: bfloat16 [4, 2048, 2048], P(None, 'row', 'col')
- coefficients: float32 [2], replicated
All inputs are finite; a program needn't handle non-finite values.
Results may differ from a plain program's by a relative error of at most 0.023.
Values may be sent and summed in bfloat16 or wider, within the bound.
A program may use at most 64 MiB of HBM per device.

v0:
```python
import jax
import jax.numpy as jnp
from jax import lax
from jax.sharding import PartitionSpec as P

epsilon = 1e-06


def coupling(left_tensor, right_tensor):
    channels = left_tensor.shape[0]
    joined = jnp.einsum(
        "wuac,uvbd->vabwcd", left_tensor, right_tensor, precision=lax.Precision.HIGHEST
    )
    return joined.reshape(channels, 4, channels, 4)


def contract_left(portion, columns):
    return jnp.einsum("wax,txb->wtba", portion, columns, preferred_element_type=jnp.float32)


def mix_channels(coupling_table, cross):
    mixed_bond = jnp.einsum(
        "vswt,wtba->vsba", coupling_table, cross, precision=lax.Precision.HIGHEST
    )
    return mixed_bond.astype(jnp.bfloat16)


def contract_right(mixed_bond, portion):
    return jnp.einsum("vsba,vbc->sac", mixed_bond, portion, preferred_element_type=jnp.float32)


def apply_hamiltonian(vector, coupling_table, panels):
    columns = lax.all_gather(vector, "row", axis=1, tiled=True)
    cross = contract_left(panels[0], columns)
    mixed_bond = mix_channels(coupling_table, cross)
    partials = contract_right(mixed_bond, panels[1])
    return lax.psum_scatter(
        partials.astype(jnp.bfloat16), "col", scatter_dimension=2, tiled=True
    ).astype(jnp.float32)


def local_mean(former, latter, entries):
    return jnp.sum(former * latter) / entries


def body(start_vector, left_env, right_env, left_tensor, right_tensor):
    coupling_table = coupling(left_tensor, right_tensor)
    entries = float(
        start_vector.shape[0]
        * start_vector.shape[1]
        * start_vector.shape[2]
        * lax.axis_size("row")
        * lax.axis_size("col")
    )
    panels = (
        lax.all_gather(left_env, "col", axis=2, tiled=True),
        lax.all_gather(right_env, "row", axis=2, tiled=True),
    )
    base_vector = start_vector.astype(jnp.float32)
    image = apply_hamiltonian(start_vector, coupling_table, panels)
    base_square, correlation, image_square = lax.psum(
        (
            local_mean(base_vector, base_vector, entries),
            local_mean(base_vector, image, entries),
            local_mean(image, image, entries),
        ),
        ("row", "col"),
    )
    alpha = correlation / (base_square + epsilon)
    residual = image - alpha * base_vector
    rho = jnp.sqrt(image_square - 2.0 * alpha * correlation + alpha * alpha * base_square + epsilon)
    next_vector = (residual / rho).astype(jnp.bfloat16)
    coefficients = jnp.stack([alpha, rho])
    return (next_vector, coefficients)


def solution(mesh):
    return jax.shard_map(
        body,
        mesh=mesh,
        in_specs=(P(None, "row", "col"), P(None, "row", "col"), P(None, "col", "row"), P(), P()),
        out_specs=(P(None, "row", "col"), P()),
        check_vma=False,
    )
```

profile of v0, /device:TPU:12, one launch (start us, length us, event | category | flops | bytes accessed | tf_op | source)
XLA Modules:
  0.0 411.1 jit_solution(12811330662160053242)
XLA Ops:
  7.2 0.0 copy-start
  7.2 0.0 copy-start.2
  7.2 0.0 all-gather.4.cloned.1.call-start
  7.2 2.3 copy.15
  9.5 0.0 all-gather.4.cloned.1.call-update
  9.5 0.0 all-gather.6.cloned.1.call-start
  9.6 0.7 all-gather.6.cloned.1.call-update
  10.3 0.0 all-gather.8.cloned.1.call-start
  10.3 0.7 all-gather.8.cloned.1.call-update
  11.0 0.0 reduce-scatter.2.cloned.1.call-start
  11.1 0.0 copy-done
  11.1 0.0 copy-done.2
  11.1 0.4 convolution_bitcast_fusion
  11.6 52.4 %all-gather.4.cloned.1.call-done = bf16[4,2048,256]{1,2,0:T(8,128)(2,1)} async-done(((bf16[4,512,256]{1,2,0:T(8,128)(2,1)}), bf16[4,2048,256]{1,2,0:T(8,128)(2,1)}) %all-gather.4.cloned.1.call-update) | async-done | bytes 4194320 | tf_op jit(solution)/shard_map/all_gather | solution.py:33
  64.0 98.7 %all-gather.6.cloned.1.call-done = bf16[5,512,2048]{2,1,0:T(8,128)(2,1)} async-done(((bf16[5,512,256]{2,1,0:T(8,128)(2,1)}), bf16[5,512,2048]{2,1,0:T(8,128)(2,1)}) %all-gather.6.cloned.1.call-update) | async-done | bytes 10485776 | tf_op jit(solution)/shard_map/all_gather | solution.py:56
  162.7 15.1 %fusion.10 = f32[5,4,256,512]{3,2,0,1:T(8,128)S(1)} fusion(bf16[5,512,2048]{2,1,0:T(8,128)(2,1)} %all-gather.6.cloned.1.call-done, bf16[4,2048,256]{1,2,0:T(8,128)(2,1)} %all-gather.4.cloned.1.call-done), kind=kOutput, calls=%fused_computation.10 | convolution fusion | flops 10737418240 | bytes 25165824 | tf_op jit(solution)/shard_map/wax,txb->wtba/dot_general | solution.py:18
  177.7 66.0 %bitcast_convert_fusion.1 = bf16[5,4,256,512]{3,0,2,1:T(8,128)(2,1)} fusion(f32[5,4,256,512]{3,2,0,1:T(8,128)S(1)} %fusion.10, f32[5,4,5,4,1]{2,3,1,0,4:T(4,128)S(1)} %bitcast.38), kind=kOutput, calls=%fused_computation.1 | convolution fusion | flops 631767040 | bytes 15730240 | tf_op jit(solution)/shard_map/vswt,wtba->vsba/dot_general | solution.py:22
  243.7 0.0 all-gather.8.cloned.1.call-done
  243.7 19.3 %bitcast_convert_fusion = bf16[4,512,2048]{2,1,0:T(8,128)(2,1)} fusion(bf16[5,256,2048]{2,1,0:T(8,128)(2,1)} %all-gather.8.cloned.1.call-done, bf16[5,4,256,512]{3,0,2,1:T(8,128)(2,1)} %bitcast_convert_fusion.1), kind=kOutput, calls=%fused_computation | convolution fusion | flops 10741612544 | bytes 18874368 | tf_op jit(solution)/shard_map/vsba,vbc->sac/dot_general | solution.py:29
  263.0 0.0 copy-start.1
  263.0 0.0 reduce-scatter.2.cloned.1.call-update
  263.0 87.8 %reduce-scatter.2.cloned.1.call-done = bf16[4,512,256]{2,1,0:T(8,128)(2,1)} async-done(((bf16[4,512,2048]{2,1,0:T(8,128)(2,1)}), bf16[4,512,256]{2,1,0:T(8,128)(2,1)}) %reduce-scatter.2.cloned.1.call-update) | async-done | bytes 1048592 | tf_op jit(solution)/shard_map/reduce_scatter | solution.py:37
  350.8 0.0 copy-done.1
  350.8 2.5 fusion.19
  355.3 43.0 %all-reduce = (f32[]{:T(128)}, f32[]{:T(128)}, f32[]{:T(128)}) all-reduce(f32[]{:T(128)S(6)} %div.21, f32[]{:T(128)S(6)} %div.18, f32[]{:T(128)S(6)} %div.19), channel_id=1, replica_groups=mesh['row'=4,'col'=8] {'row','col'}, use_global_device_ids=true, to_apply=%region_6.0 | all-reduce | flops 3 | bytes 24 | tf_op jit(solution)/shard_map/psum | solution.py:61
  401.4 0.6 pad_maximum_fusion
  402.0 2.6 fusion.16
  (1 shorter events, 0.0 us)
Async XLA Ops:
  7.2 3.9 copy-start
  7.2 3.9 copy-start.2
  7.2 56.8 %all-gather.4.cloned.1.call-start = ((), (), s32[]{:S(2)}) async-start(), calls=%async_computation.1 | async-start | bytes 5242880 | tf_op jit(solution)/shard_map/all_gather | solution.py:33
  9.5 153.1 %all-gather.6.cloned.1.call-start = ((), (), s32[]{:S(2)}) async-start(), calls=%async_computation.2 | async-start | bytes 11796480 | tf_op jit(solution)/shard_map/all_gather | solution.py:56
  10.3 233.4 %all-gather.8.cloned.1.call-start = ((), (), s32[]{:S(2)}) async-start(), calls=%async_computation.3 | async-start | bytes 6553600 | tf_op jit(solution)/shard_map/all_gather | solution.py:57
  11.0 339.8 %reduce-scatter.2.cloned.1.call-start = ((), (), s32[]{:S(2)}) async-start(), calls=%async_computation.4 | async-start | bytes 9437184 | tf_op jit(solution)/shard_map/reduce_scatter | solution.py:37
  263.0 87.8 %copy-start.1 = (bf16[4,512,256]{2,1,0:T(8,128)(2,1)S(1)}, bf16[4,512,256]{2,1,0:T(8,128)(2,1)}, u32[]{:S(2)}) copy-start(bf16[4,512,256]{2,1,0:T(8,128)(2,1)} %param.5) | copy-start | bytes 3145732
Sparse Core Ops, SparseCore 0:
  10.4 53.5 all-gather.3
  65.6 97.0 all-gather.5
  164.5 62.0 all-gather.7
  263.2 87.6 reduce-scatter.1
where the time goes:
time: 411 us
  waiting for transfers between devices  240 us (58%)
  matrix products  101 us (25%)
  blocking collectives  43 us (10%)
  between operations  19 us (5%)
  other arithmetic  5.64 us (1%)
    all_gather x1, waiting for transfers between devices, body(): lax.all_gather(left_env, 'col', axis=2, tiled=True)  98.7 us
    reduce_scatter x1, waiting for transfers between devices, apply_hamiltonian(): lax.psum_scatter(partials.astype(jnp.bfloat16), 'col', scatter_dimension=...  87.8 us
    dot_general x1, matrix products, mix_channels(): jnp.einsum('vswt,wtba->vsba', coupling_table, cross, precision=lax.Precis...  66 us
    all_gather x1, waiting for transfers between devices, apply_hamiltonian(): columns = lax.all_gather(vector, 'row', axis=1, tiled=True)  52.4 us
    psum x1, blocking collectives, body(): lax.psum((local_mean(base_vector, base_vector, entries), local_mean(base_...  43 us
    dot_general x1, matrix products, contract_right(): jnp.einsum('vsba,vbc->sac', mixed_bond, portion, preferred_element_type=j...  19.3 us
    dot_general x1, matrix products, contract_left(): jnp.einsum('wax,txb->wtba', portion, columns, preferred_element_type=jnp....  15.1 us
  transfers between devices with their start and end apart: 4, of which 3 were waited for; matrix products, arithmetic and copies ran while one was open for 20% of the time, Pallas kernels for 0%

commit v1 on v0

--- a/solution.py
+++ b/solution.py
@@ -30,7 +30,12 @@
 
 
 def apply_hamiltonian(vector, coupling_table, panels):
-    columns = lax.all_gather(vector, "row", axis=1, tiled=True)
+    ring = [vector]
+    for hop in range(3):
+        ring.append(lax.ppermute(ring[-1], "row", [(dev, (dev + 1) % 4) for dev in range(4)]))
+    columns = jnp.roll(
+        jnp.concatenate(ring[::-1], axis=1), (lax.axis_index("row") + 1) * ring[0].shape[1], axis=1
+    )
     cross = contract_left(panels[0], columns)
     mixed_bond = mix_channels(coupling_table, cross)
     partials = contract_right(mixed_bond, panels[1])

time: 411 us -> 357 us (0.87)
  waiting for transfers between devices: 240 us -> 172 us
  local copies, waits for them, and re-layouts: 2.33 us -> 12.9 us
    all_gather x1, waiting for transfers between devices: 98.7 us -> 11.7 us  [body(): lax.all_gather(left_env, 'col', axis=2, tiled=True)]
    ppermute x0 -> x3, waiting for transfers between devices: none -> 71.9 us  [apply_hamiltonian(): lax.ppermute(ring[-1], 'row', [(dev, (dev + 1) % 4) for dev in range(4)])]
    all_gather x1 -> x0, waiting for transfers between devices: 52.4 us -> none  [apply_hamiltonian(): columns = lax.all_gather(vector, 'row', axis=1, tiled=True)]
    unnamed x7 -> x12, local copies, waits for them, and re-layouts: 2.29 us -> 11.8 us
  transfers between devices with their start and end apart: 4 -> 6, of which waited for: 3 -> 5; matrix products, arithmetic and copies ran while one was open for 20% -> 27% of each run, Pallas kernels for 0% -> 0%
where the time goes in v1:
time: 357 us; the launch traced here: 356 us
  waiting for transfers between devices  172 us (48%)
  matrix products  101 us (28%)
  blocking collectives  43 us (12%)
  between operations  19 us (5%)
  local copies, waits for them, and re-layouts  12.9 us (4%)
  other arithmetic  5.61 us (2%)
    reduce_scatter x1, waiting for transfers between devices, apply_hamiltonian(): lax.psum_scatter(partials.astype(jnp.bfloat16), 'col', scatter_dimension=...  87.8 us
    ppermute x3, waiting for transfers between devices, apply_hamiltonian(): lax.ppermute(ring[-1], 'row', [(dev, (dev + 1) % 4) for dev in range(4)])  71.9 us
    dot_general x1, matrix products, mix_channels(): jnp.einsum('vswt,wtba->vsba', coupling_table, cross, precision=lax.Precis...  66 us
    psum x1, blocking collectives, body(): lax.psum((local_mean(base_vector, base_vector, entries), local_mean(base_...  43 us
    dot_general x1, matrix products, contract_right(): jnp.einsum('vsba,vbc->sac', mixed_bond, portion, preferred_element_type=j...  19.3 us
    dot_general x1, matrix products, contract_left(): jnp.einsum('wax,txb->wtba', portion, columns, preferred_element_type=jnp....  15.1 us
    unnamed x12, local copies, waits for them, and re-layouts  11.8 us
    all_gather x1, waiting for transfers between devices, body(): lax.all_gather(left_env, 'col', axis=2, tiled=True)  11.7 us
  transfers between devices with their start and end apart: 6, of which 5 were waited for; matrix products, arithmetic and copies ran while one was open for 27% of the time, Pallas kernels for 0%

profile of v1, /device:TPU:12, one launch (start us, length us, event | category | flops | bytes accessed | tf_op | source)
XLA Modules:
  0.0 356.3 jit_solution(4056390217884464923)
XLA Ops:
  7.2 0.0 copy-start
  7.2 0.0 all-gather.3.cloned.1.call-start
  7.2 0.7 all-gather.3.cloned.1.call-update
  7.9 0.0 all-gather.5.cloned.1.call-start
  8.0 1.5 copy.15
  9.5 1.5 collective-permute-start
  11.0 0.0 all-gather.5.cloned.1.call-update
  11.0 0.0 reduce-scatter.2.cloned.1.call-start
  11.1 24.2 %collective-permute-done = bf16[4,512,256]{1,2,0:T(8,128)(2,1)S(1)} collective-permute-done((bf16[4,512,256]{1,2,0:T(8,128)(2,1)S(1)}, bf16[4,512,256]{1,2,0:T(8,128)(2,1)S(1)}, u32[]{:S(2)}, u32[]{:S(2)}) %collective-permute-start) | collective-permute-done | bytes 1048608 | tf_op jit(solution)/shard_map/ppermute | solution.py:35
  35.3 0.6 collective-permute-start.1
  35.9 24.5 %collective-permute-done.1 = bf16[4,512,256]{1,2,0:T(8,128)(2,1)S(1)} collective-permute-done((bf16[4,512,256]{1,2,0:T(8,128)(2,1)S(1)}, bf16[4,512,256]{1,2,0:T(8,128)(2,1)S(1)}, u32[]{:S(2)}, u32[]{:S(2)}) %collective-permute-start.1) | collective-permute-done | bytes 1048608 | tf_op jit(solution)/shard_map/ppermute | solution.py:35
  60.4 0.0 collective-permute-start.2
  60.4 0.0 copy-done
  60.4 1.1 convolution_bitcast_fusion
  61.5 23.2 %collective-permute-done.2 = bf16[4,512,256]{1,2,0:T(8,128)(2,1)} collective-permute-done((bf16[4,512,256]{1,2,0:T(8,128)(2,1)S(1)}, bf16[4,512,256]{1,2,0:T(8,128)(2,1)}, u32[]{:S(2)}, u32[]{:S(2)}) %collective-permute-start.2) | collective-permute-done | bytes 1048608 | tf_op jit(solution)/shard_map/ppermute | solution.py:35
  84.8 2.3 constant_dynamic-update-slice_fusion.7
  87.1 1.1 constant_dynamic-update-slice_fusion.6
  88.2 1.1 constant_dynamic-update-slice_fusion.5
  89.3 1.1 constant_dynamic-update-slice_fusion.4
  90.5 2.3 constant_dynamic-update-slice_fusion.3
  92.8 1.1 constant_dynamic-update-slice_fusion.2
  93.9 1.1 constant_dynamic-update-slice_fusion.1
  95.0 1.1 constant_dynamic-update-slice_fusion
  96.1 11.7 %all-gather.3.cloned.1.call-done = bf16[5,512,2048]{2,1,0:T(8,128)(2,1)} async-done(((bf16[5,512,256]{2,1,0:T(8,128)(2,1)}), bf16[5,512,2048]{2,1,0:T(8,128)(2,1)}) %all-gather.3.cloned.1.call-update) | async-done | bytes 10485776 | tf_op jit(solution)/shard_map/all_gather | solution.py:61
  107.8 15.1 %fusion.11 = f32[5,4,256,512]{3,2,0,1:T(8,128)S(1)} fusion(bf16[5,512,2048]{2,1,0:T(8,128)(2,1)} %all-gather.3.cloned.1.call-done, bf16[4,4096,256]{1,2,0:T(8,128)(2,1)} %constant_dynamic-update-slice_fusion, s32[]{:T(128)S(6)} %select_n.14), kind=kOutput, calls=%fused_computation.11 | convolution fusion | flops 10737418240 | bytes 25165828 | tf_op jit(solution)/shard_map/wax,txb->wtba/dot_general | solution.py:18
  122.8 66.0 %bitcast_convert_fusion.1 = bf16[5,4,256,512]{3,0,2,1:T(8,128)(2,1)} fusion(f32[5,4,256,512]{3,2,0,1:T(8,128)S(1)} %fusion.11, f32[5,4,5,4,1]{2,3,1,0,4:T(4,128)S(1)} %bitcast.38), kind=kOutput, calls=%fused_computation.1 | convolution fusion | flops 631767040 | bytes 15730240 | tf_op jit(solution)/shard_map/vswt,wtba->vsba/dot_general | solution.py:22
  188.8 0.0 all-gather.5.cloned.1.call-done
  188.8 19.3 %bitcast_convert_fusion = bf16[4,512,2048]{2,1,0:T(8,128)(2,1)} fusion(bf16[5,256,2048]{2,1,0:T(8,128)(2,1)} %all-gather.5.cloned.1.call-done, bf16[5,4,256,512]{3,0,2,1:T(8,128)(2,1)} %bitcast_convert_fusion.1), kind=kOutput, calls=%fused_computation | convolution fusion | flops 10741612544 | bytes 18874368 | tf_op jit(solution)/shard_map/vsba,vbc->sac/dot_general | solution.py:29
  208.1 0.0 copy-start.1
  208.1 0.0 reduce-scatter.2.cloned.1.call-update
  208.1 87.8 %reduce-scatter.2.cloned.1.call-done = bf16[4,512,256]{2,1,0:T(8,128)(2,1)} async-done(((bf16[4,512,2048]{2,1,0:T(8,128)(2,1)}), bf16[4,512,256]{2,1,0:T(8,128)(2,1)}) %reduce-scatter.2.cloned.1.call-update) | async-done | bytes 1048592 | tf_op jit(solution)/shard_map/reduce_scatter | solution.py:42
  296.0 0.0 copy-done.1
  296.0 2.4 fusion.20
  300.3 43.0 %all-reduce = (f32[]{:T(128)}, f32[]{:T(128)}, f32[]{:T(128)}) all-reduce(f32[]{:T(128)S(6)} %div.21, f32[]{:T(128)S(6)} %div.18, f32[]{:T(128)S(6)} %div.19), channel_id=1, replica_groups=mesh['row'=4,'col'=8] {'row','col'}, use_global_device_ids=true, to_apply=%region_6.7 | all-reduce | flops 3 | bytes 24 | tf_op jit(solution)/shard_map/psum | solution.py:66
  346.6 0.6 pad_maximum_fusion
  347.2 2.6 fusion.17
  (1 shorter events, 0.0 us)
Async XLA Ops:
  7.2 53.2 %copy-start = (f32[5,5,2,2]{1,3,2,0:T(2,128)S(1)}, f32[5,5,2,2]{1,3,2,0:T(2,128)}, u32[]{:S(2)}) copy-start(f32[5,5,2,2]{1,3,2,0:T(2,128)} %param.8) | copy-start | bytes 1204
  7.2 100.6 %all-gather.3.cloned.1.call-start = ((), (), s32[]{:S(2)}) async-start(), calls=%async_computation.1 | async-start | bytes 11796480 | tf_op jit(solution)/shard_map/all_gather | solution.py:61
  7.9 180.9 %all-gather.5.cloned.1.call-start = ((), (), s32[]{:S(2)}) async-start(), calls=%async_computation.2 | async-start | bytes 6553600 | tf_op jit(solution)/shard_map/all_gather | solution.py:62
  9.5 25.9 %collective-permute-start = (bf16[4,512,256]{1,2,0:T(8,128)(2,1)S(1)}, bf16[4,512,256]{1,2,0:T(8,128)(2,1)S(1)}, u32[]{:S(2)}, u32[]{:S(2)}) collective-permute-start(bf16[4,512,256]{1,2,0:T(8,128)(2,1)S(1)} %copy.15), channel_id=1, source_target_pairs={{0,8},{8,16},{16,24},{24,0},{1,9},{9,17},{17,25},{25,1},{2,10},{10... | collective-permute-start | bytes 3145736 | tf_op jit(solution)/shard_map/ppermute | solution.py:35
  11.0 284.9 %reduce-scatter.2.cloned.1.call-start = ((), (), s32[]{:S(2)}) async-start(), calls=%async_computation.3 | async-start | bytes 9437184 | tf_op jit(solution)/shard_map/reduce_scatter | solution.py:42
  35.3 25.0 %collective-permute-start.1 = (bf16[4,512,256]{1,2,0:T(8,128)(2,1)S(1)}, bf16[4,512,256]{1,2,0:T(8,128)(2,1)S(1)}, u32[]{:S(2)}, u32[]{:S(2)}) collective-permute-start(bf16[4,512,256]{1,2,0:T(8,128)(2,1)S(1)} %collective-permute-done), channel_id=1, source_target_pairs={{0,8},{8,16},{16,24},{24,0},{1,9},{9,17},{17,25},{25,1},{2,10},{10... | collective-permute-start | bytes 3145736 | tf_op jit(solution)/shard_map/ppermute | solution.py:35
  60.4 24.4 %collective-permute-start.2 = (bf16[4,512,256]{1,2,0:T(8,128)(2,1)S(1)}, bf16[4,512,256]{1,2,0:T(8,128)(2,1)}, u32[]{:S(2)}, u32[]{:S(2)}) collective-permute-start(bf16[4,512,256]{1,2,0:T(8,128)(2,1)S(1)} %collective-permute-done.1), channel_id=1, source_target_pairs={{0,8},{8,16},{16,24},{24,0},{1,9},{9,17},{17,25},{25,1},{2,10},{10... | collective-permute-start | bytes 3145736 | tf_op jit(solution)/shard_map/ppermute | solution.py:35
  208.1 87.9 %copy-start.1 = (bf16[4,512,256]{2,1,0:T(8,128)(2,1)S(1)}, bf16[4,512,256]{2,1,0:T(8,128)(2,1)}, u32[]{:S(2)}) copy-start(bf16[4,512,256]{2,1,0:T(8,128)(2,1)} %param.5) | copy-start | bytes 3145732
Sparse Core Ops, SparseCore 0:
  9.6 98.1 all-gather.2
  109.6 62.0 all-gather.4
  208.3 87.6 reduce-scatter.1

commit v2 on v0

--- a/solution.py
+++ b/solution.py
@@ -59,12 +59,15 @@
     base_vector = start_vector.astype(jnp.float32)
     image = apply_hamiltonian(start_vector, coupling_table, panels)
     base_square, correlation, image_square = lax.psum(
-        (
-            local_mean(base_vector, base_vector, entries),
-            local_mean(base_vector, image, entries),
-            local_mean(image, image, entries),
+        lax.psum(
+            (
+                local_mean(base_vector, base_vector, entries),
+                local_mean(base_vector, image, entries),
+                local_mean(image, image, entries),
+            ),
+            "col",
         ),
-        ("row", "col"),
+        "row",
     )
     alpha = correlation / (base_square + epsilon)
     residual = image - alpha * base_vector

time: 411 us -> 398 us (0.968); the launches traced: 411 us -> 391 us
  blocking collectives: 43 us -> 23.2 us
    psum x1, blocking collectives: 43 us -> 13.6 us  [body(): lax.psum((local_mean(base_vector, base_vector, entries), local_mean(base_...]
    psum x0 -> x1, blocking collectives: none -> 9.57 us  [body(): lax.psum(lax.psum((local_mean(base_vector, base_vector, entries), local_m...]
  transfers between devices with their start and end apart: 4 -> 4, of which waited for: 3 -> 3; matrix products, arithmetic and copies ran while one was open for 20% -> 21% of each run, Pallas kernels for 0% -> 0%
where the time goes in v2:
time: 398 us; the launch traced here: 391 us
  waiting for transfers between devices  240 us (60%)
  matrix products  101 us (25%)
  blocking collectives  23.2 us (6%)
  between operations  18.9 us (5%)
  other arithmetic  5.58 us (1%)
    all_gather x1, waiting for transfers between devices, body(): lax.all_gather(left_env, 'col', axis=2, tiled=True)  98.7 us
    reduce_scatter x1, waiting for transfers between devices, apply_hamiltonian(): lax.psum_scatter(partials.astype(jnp.bfloat16), 'col', scatter_dimension=...  87.8 us
    dot_general x1, matrix products, mix_channels(): jnp.einsum('vswt,wtba->vsba', coupling_table, cross, precision=lax.Precis...  66 us
    all_gather x1, waiting for transfers between devices, apply_hamiltonian(): columns = lax.all_gather(vector, 'row', axis=1, tiled=True)  52.4 us
    dot_general x1, matrix products, contract_right(): jnp.einsum('vsba,vbc->sac', mixed_bond, portion, preferred_element_type=j...  19.3 us
    dot_general x1, matrix products, contract_left(): jnp.einsum('wax,txb->wtba', portion, columns, preferred_element_type=jnp....  15.1 us
    psum x1, blocking collectives, body(): lax.psum((local_mean(base_vector, base_vector, entries), local_mean(base_...  13.6 us
    psum x1, blocking collectives, body(): lax.psum(lax.psum((local_mean(base_vector, base_vector, entries), local_m...  9.57 us
  transfers between devices with their start and end apart: 4, of which 3 were waited for; matrix products, arithmetic and copies ran while one was open for 21% of the time, Pallas kernels for 0%

profile of v2, /device:TPU:12, one launch (start us, length us, event | category | flops | bytes accessed | tf_op | source)
XLA Modules:
  0.0 391.3 jit_solution(2774186295418766670)
XLA Ops:
  7.2 0.0 copy-start
  7.2 0.0 copy-start.2
  7.2 0.0 all-gather.4.cloned.1.call-start
  7.2 2.3 copy.15
  9.5 0.0 all-gather.4.cloned.1.call-update
  9.5 0.0 all-gather.6.cloned.1.call-start
  9.6 0.7 all-gather.6.cloned.1.call-update
  10.3 0.0 all-gather.8.cloned.1.call-start
  10.3 0.7 all-gather.8.cloned.1.call-update
  11.0 0.0 reduce-scatter.2.cloned.1.call-start
  11.1 0.0 copy-done
  11.1 0.0 copy-done.2
  11.1 0.4 convolution_bitcast_fusion
  11.6 52.4 %all-gather.4.cloned.1.call-done = bf16[4,2048,256]{1,2,0:T(8,128)(2,1)} async-done(((bf16[4,512,256]{1,2,0:T(8,128)(2,1)}), bf16[4,2048,256]{1,2,0:T(8,128)(2,1)}) %all-gather.4.cloned.1.call-update) | async-done | bytes 4194320 | tf_op jit(solution)/shard_map/all_gather | solution.py:33
  64.0 98.7 %all-gather.6.cloned.1.call-done = bf16[5,512,2048]{2,1,0:T(8,128)(2,1)} async-done(((bf16[5,512,256]{2,1,0:T(8,128)(2,1)}), bf16[5,512,2048]{2,1,0:T(8,128)(2,1)}) %all-gather.6.cloned.1.call-update) | async-done | bytes 10485776 | tf_op jit(solution)/shard_map/all_gather | solution.py:56
  162.7 15.1 %fusion.10 = f32[5,4,256,512]{3,2,0,1:T(8,128)S(1)} fusion(bf16[5,512,2048]{2,1,0:T(8,128)(2,1)} %all-gather.6.cloned.1.call-done, bf16[4,2048,256]{1,2,0:T(8,128)(2,1)} %all-gather.4.cloned.1.call-done), kind=kOutput, calls=%fused_computation.10 | convolution fusion | flops 10737418240 | bytes 25165824 | tf_op jit(solution)/shard_map/wax,txb->wtba/dot_general | solution.py:18
  177.7 66.0 %bitcast_convert_fusion.1 = bf16[5,4,256,512]{3,0,2,1:T(8,128)(2,1)} fusion(f32[5,4,256,512]{3,2,0,1:T(8,128)S(1)} %fusion.10, f32[5,4,5,4,1]{2,3,1,0,4:T(4,128)S(1)} %bitcast.38), kind=kOutput, calls=%fused_computation.1 | convolution fusion | flops 631767040 | bytes 15730240 | tf_op jit(solution)/shard_map/vswt,wtba->vsba/dot_general | solution.py:22
  243.7 0.0 all-gather.8.cloned.1.call-done
  243.7 19.3 %bitcast_convert_fusion = bf16[4,512,2048]{2,1,0:T(8,128)(2,1)} fusion(bf16[5,256,2048]{2,1,0:T(8,128)(2,1)} %all-gather.8.cloned.1.call-done, bf16[5,4,256,512]{3,0,2,1:T(8,128)(2,1)} %bitcast_convert_fusion.1), kind=kOutput, calls=%fused_computation | convolution fusion | flops 10741612544 | bytes 18874368 | tf_op jit(solution)/shard_map/vsba,vbc->sac/dot_general | solution.py:29
  263.0 0.0 copy-start.1
  263.0 0.0 reduce-scatter.2.cloned.1.call-update
  263.1 87.8 %reduce-scatter.2.cloned.1.call-done = bf16[4,512,256]{2,1,0:T(8,128)(2,1)} async-done(((bf16[4,512,2048]{2,1,0:T(8,128)(2,1)}), bf16[4,512,256]{2,1,0:T(8,128)(2,1)}) %reduce-scatter.2.cloned.1.call-update) | async-done | bytes 1048592 | tf_op jit(solution)/shard_map/reduce_scatter | solution.py:37
  350.9 0.0 copy-done.1
  350.9 2.4 fusion.19
  355.2 13.6 %all-reduce = (f32[]{:T(128)}, f32[]{:T(128)}, f32[]{:T(128)}) all-reduce(f32[]{:T(128)S(6)} %div.21, f32[]{:T(128)S(6)} %div.18, f32[]{:T(128)S(6)} %div.19), channel_id=1, replica_groups=mesh['row'=4,'col'=8] {'col'}, use_global_device_ids=true, to_apply=%region_8.0 | all-reduce | flops 3 | bytes 24 | tf_op jit(solution)/shard_map/psum | solution.py:62
  368.8 9.6 %all-reduce.1 = (f32[]{:T(128)}, f32[]{:T(128)}, f32[]{:T(128)}) all-reduce(f32[]{:T(128)} %get-tuple-element.5, f32[]{:T(128)} %get-tuple-element.6, f32[]{:T(128)} %get-tuple-element.7), channel_id=1, replica_groups=mesh['row'=4,'col'=8] {'row'}, use_global_device_ids=true, to_apply=%region_9.0 | all-reduce | flops 3 | bytes 24 | tf_op jit(solution)/shard_map/psum | solution.py:61
  381.6 0.6 pad_maximum_fusion
  382.2 2.6 fusion.16
  (1 shorter events, 0.0 us)
Async XLA Ops:
  7.2 3.9 copy-start
  7.2 3.9 copy-start.2
  7.2 56.8 %all-gather.4.cloned.1.call-start = ((), (), s32[]{:S(2)}) async-start(), calls=%async_computation.1 | async-start | bytes 5242880 | tf_op jit(solution)/shard_map/all_gather | solution.py:33
  9.5 153.1 %all-gather.6.cloned.1.call-start = ((), (), s32[]{:S(2)}) async-start(), calls=%async_computation.2 | async-start | bytes 11796480 | tf_op jit(solution)/shard_map/all_gather | solution.py:56
  10.3 233.4 %all-gather.8.cloned.1.call-start = ((), (), s32[]{:S(2)}) async-start(), calls=%async_computation.3 | async-start | bytes 6553600 | tf_op jit(solution)/shard_map/all_gather | solution.py:57
  11.0 339.9 %reduce-scatter.2.cloned.1.call-start = ((), (), s32[]{:S(2)}) async-start(), calls=%async_computation.4 | async-start | bytes 9437184 | tf_op jit(solution)/shard_map/reduce_scatter | solution.py:37
  263.0 87.9 %copy-start.1 = (bf16[4,512,256]{2,1,0:T(8,128)(2,1)S(1)}, bf16[4,512,256]{2,1,0:T(8,128)(2,1)}, u32[]{:S(2)}) copy-start(bf16[4,512,256]{2,1,0:T(8,128)(2,1)} %param.5) | copy-start | bytes 3145732
Sparse Core Ops, SparseCore 0:
  10.4 53.5 all-gather.3
  65.6 97.0 all-gather.5
  164.5 62.0 all-gather.7
  263.2 87.6 reduce-scatter.1
